TPU v7x, 32 devices: a whole 2x2x4 slice. The times are simulated.
32 devices in a mesh: dp: 8 (over z, core), tensor: 4 (over y, x).
Axes of the slice: x: 2, y: 2, z: 4, core: 2. Of those that a mesh axis runs over, the one named last changes fastest.
Arguments:
- tokens: bfloat16 [4096, 2048], P('dp'), may hold values from -6 to 6
- segments: int32 [8, 512], P('dp'), may hold values from 0 to 1, never falling along the last dimension, each value on 1 to 511 neighbouring positions
- expert_ids: int32 [4096, 6], P('dp'), may hold values from 0 to 31, all different within a row; in each aligned block of 512 rows (0 to 511, 512 to 1023, ...) at most 144 rows name the same one
- route_weight: float32 [4096, 6], P('dp'), may hold values from 0.1 to 1
- norm1_gain: bfloat16 [2048], P(('dp', 'tensor')), may hold values from 0.5 to 1.5
- q_weight: bfloat16 [2048, 3072], P('dp', 'tensor'), may hold values from -0.125 to 0.125
- kva_weight: bfloat16 [2048, 576], P(('dp', 'tensor')), may hold values from -0.125 to 0.125
- kv_gain: bfloat16 [512], P(('dp', 'tensor')), may hold values from 0.5 to 1.5
- kvb_weight: bfloat16 [512, 4096], P('dp', 'tensor'), may hold values from -0.25 to 0.25
- out_weight: bfloat16 [2048, 2048], P('tensor', 'dp'), may hold values from -1 to 1
- norm2_gain: bfloat16 [2048], P(('dp', 'tensor')), may hold values from 0.5 to 1.5
- shared_gate: bfloat16 [2048, 2816], P('dp', 'tensor'), may hold values from -0.125 to 0.125
- shared_up: bfloat16 [2048, 2816], P('dp', 'tensor'), may hold values from -0.125 to 0.125
- shared_down: bfloat16 [2816, 2048], P('tensor', 'dp'), may hold values from -0.21875 to 0.21875
- expert_gate: bfloat16 [32, 2048, 1408], P('dp', None, 'tensor'), may hold values from -0.125 to 0.125
- expert_up_projection: bfloat16 [32, 2048, 1408], P('dp', None, 'tensor'), may hold values from -0.125 to 0.125
- expert_down: bfloat16 [32, 1408, 2048], P('dp', 'tensor'), may hold values from -0.3125 to 0.3125
- cotangent: bfloat16 [4096, 2048], P('dp'), may hold values from -6 to 6
Outputs:
- output: bfloat16 [4096, 2048], P('dp')
- grad_tokens: float32 [4096, 2048], P('dp')
- grad_norm1_gain: float32 [2048], P(('dp', 'tensor'))
- grad_q_weight: float32 [2048, 3072], P('dp', 'tensor')
- grad_kva_weight: float32 [2048, 576], P(('dp', 'tensor'))
- grad_kv_gain: float32 [512], P(('dp', 'tensor'))
- grad_kvb_weight: float32 [512, 4096], P('dp', 'tensor')
- grad_out_weight: float32 [2048, 2048], P('tensor', 'dp')
- grad_norm2_gain: float32 [2048], P(('dp', 'tensor'))
- grad_shared_gate: float32 [2048, 2816], P('dp', 'tensor')
- grad_shared_up: float32 [2048, 2816], P('dp', 'tensor')
- grad_shared_down: float32 [2816, 2048], P('tensor', 'dp')
- grad_expert_gate: float32 [32, 2048, 1408], P('dp', None, 'tensor')
- grad_expert_up: float32 [32, 2048, 1408], P('dp', None, 'tensor')
- grad_expert_down: float32 [32, 1408, 2048], P('dp', 'tensor')
Inputs may be any that keep to these rules, and one draw needn't show every extreme that they name: `segments`: each row holds 2 sequences laid end to end; numbers never fall along a row; each sequence has 1 to 511 tokens. `expert_ids`: each token names 6 different experts; among the 512 tokens of one index of dp no expert is named more than 144 times, a bound that some block reaches.
All inputs are finite; a program needn't handle non-finite values.
Results may differ from a plain program's by a relative error of at most 0.025.
Values may be sent and summed in bfloat16 or wider, within the bound.
A program may use at most 384 MiB of HBM per device.

v0:
```python
import jax
import jax.numpy as jnp
from jax import lax
from jax.sharding import PartitionSpec as P

NOPE = 128
ROPE = 64
VDIM = 128
LATENT = 512
SEGS = 2


epsilon = 1e-06
theta_base = 10000.0


def dot_last(left, right):
    return lax.dot_general(
        left,
        right,
        (((left.ndim - 1,), (right.ndim - 1,)), ((), ())),
        preferred_element_type=jnp.float32,
    )


def dot_first(left, right):
    return lax.dot_general(
        left, right, (((0,), (0,)), ((), ())), preferred_element_type=jnp.float32
    )


def rotate(vector, cosine, sine_part):
    half_width = vector.shape[-1] // 2
    lower_half = vector[..., :half_width]
    upper_half = vector[..., half_width:]
    return jnp.concatenate(
        [
            lower_half * cosine - upper_half * sine_part,
            upper_half * cosine + lower_half * sine_part,
        ],
        axis=-1,
    )


def angles(segment_row):
    seq_len = segment_row.shape[0]
    member = segment_row[:, None] == jnp.arange(SEGS, dtype=jnp.int32)[None, :]
    seq_sizes = jnp.sum(member.astype(jnp.int32), axis=0)
    starts = jnp.cumsum(seq_sizes) - seq_sizes
    seq_first = jnp.sum(jnp.where(member, starts[None, :], 0), axis=1)
    seq_place = (jnp.arange(seq_len, dtype=jnp.int32) - seq_first).astype(jnp.float32)
    inv_freq = theta_base ** (-2.0 * jnp.arange(ROPE // 2, dtype=jnp.float32) / ROPE)
    angle_all = seq_place[:, None] * inv_freq[None, :]
    return (jnp.cos(angle_all), jnp.sin(angle_all))


def norm_scale(vector):
    return lax.rsqrt(jnp.mean(vector * vector, axis=-1, keepdims=True) + epsilon)


def norm_back(grad_hat, hat_value, inv_root):
    return inv_root * (
        grad_hat - hat_value * jnp.mean(grad_hat * hat_value, axis=-1, keepdims=True)
    )


def swish_derivative(grad_act, gate_act, up_act):
    sigma = jax.nn.sigmoid(gate_act)
    return (
        grad_act * up_act * sigma * (1.0 + gate_act * (1.0 - sigma)),
        grad_act * gate_act * sigma,
    )


def to_experts(buffer, rank_count, local_experts, capacity):
    model_width = buffer.shape[1]
    moved = lax.all_to_all(
        buffer.reshape(rank_count, local_experts * capacity, model_width),
        "dp",
        split_axis=0,
        concat_axis=0,
        tiled=True,
    )
    return moved.reshape(rank_count, local_experts, capacity, model_width)


def from_experts(partial_value, capacity):
    rank_count, local_experts, slot_count, model_width = partial_value.shape
    moved = lax.all_to_all(
        partial_value.reshape(rank_count, local_experts * capacity, model_width),
        "dp",
        split_axis=0,
        concat_axis=0,
        tiled=True,
    )
    return (moved.reshape(rank_count * local_experts * capacity, model_width), capacity, 0)


def pick_rows(row_block, flat_ids, slot_rank, per_expert, row_start, pair_weight, length, choose):
    local_rank = slot_rank - row_start
    is_valid = (local_rank >= 0) & (local_rank < per_expert)
    row_index = flat_ids * per_expert + jnp.clip(local_rank, 0, per_expert - 1)
    picked = (
        row_block[row_index].astype(jnp.float32) * jnp.where(is_valid, pair_weight, 0.0)[:, None]
    )
    return jnp.sum(picked.reshape(length, choose, row_block.shape[1]), axis=1)


def local(
    tokens,
    segments,
    expert_ids,
    route_weight,
    norm1_gain,
    q_weight,
    kva_weight,
    kv_gain,
    kvb_weight,
    out_weight,
    norm2_gain,
    shared_gate,
    shared_up,
    shared_down,
    expert_gate,
    expert_up_projection,
    expert_down,
    cotangent,
):
    length = tokens.shape[0]
    model_width = tokens.shape[1]
    groups = lax.axis_size("tensor")
    rank_count = lax.axis_size("dp")
    local_experts = expert_gate.shape[0]
    experts_all = local_experts * rank_count
    choose = expert_ids.shape[1]
    capacity = groups * -(-(3 * length * choose) // (2 * experts_all * groups))
    head_count = q_weight.shape[1] // (NOPE + ROPE)
    score_scale = (NOPE + ROPE) ** (-0.5)
    query_full, expand_full, output_full, gate_full, lift_full, lower_full = (
        lax.all_gather(q_weight, "dp", axis=0, tiled=True),
        lax.all_gather(kvb_weight, "dp", axis=0, tiled=True),
        lax.all_gather(out_weight, "dp", axis=1, tiled=True),
        lax.all_gather(shared_gate, "dp", axis=0, tiled=True),
        lax.all_gather(shared_up, "dp", axis=0, tiled=True),
        lax.all_gather(shared_down, "dp", axis=1, tiled=True),
    )
    latent_full, attention_norm_scale, latent_norm_scale, feedforward_norm_scale = (
        lax.all_gather(kva_weight, ("dp", "tensor"), axis=0, tiled=True),
        lax.all_gather(norm1_gain, ("dp", "tensor"), axis=0, tiled=True),
        lax.all_gather(kv_gain, ("dp", "tensor"), axis=0, tiled=True),
        lax.all_gather(norm2_gain, ("dp", "tensor"), axis=0, tiled=True),
    )
    attention_norm_scale = attention_norm_scale.astype(jnp.float32)
    latent_norm_scale = latent_norm_scale.astype(jnp.float32)
    feedforward_norm_scale = feedforward_norm_scale.astype(jnp.float32)
    residual_stream = tokens.astype(jnp.float32)
    inv_one = norm_scale(residual_stream)
    hat_one = residual_stream * inv_one
    normed_one = (hat_one * attention_norm_scale).astype(jnp.bfloat16)
    segment_row = segments[0]
    cosine, sine_part = angles(segment_row)
    queries = jnp.dot(normed_one, query_full, preferred_element_type=jnp.float32).reshape(
        length, head_count, NOPE + ROPE
    )
    q_rot = jnp.concatenate(
        [
            queries[..., :NOPE],
            rotate(queries[..., NOPE:], cosine[:, None, :], sine_part[:, None, :]),
        ],
        axis=-1,
    ).astype(jnp.bfloat16)
    compressed = jnp.dot(normed_one, latent_full, preferred_element_type=jnp.float32)
    latent_raw = compressed[:, :LATENT]
    inv_kv = norm_scale(latent_raw)
    hat_kv = latent_raw * inv_kv
    latent_low = (hat_kv * latent_norm_scale).astype(jnp.bfloat16)
    key_rot = rotate(compressed[:, LATENT:], cosine, sine_part).astype(jnp.bfloat16)
    keyval = (
        jnp.dot(latent_low, expand_full, preferred_element_type=jnp.float32)
        .astype(jnp.bfloat16)
        .reshape(length, head_count, NOPE + VDIM)
    )
    key_nope = keyval[..., :NOPE]
    values = keyval[..., NOPE:]
    positions = jnp.arange(length, dtype=jnp.int32)
    allowed = (segment_row[:, None] == segment_row[None, :]) & (
        positions[None, :] <= positions[:, None]
    )

    def raw_scores():
        dots = jnp.einsum(
            "thd,shd->hts", q_rot[..., :NOPE], key_nope, preferred_element_type=jnp.float32
        )
        dots = dots + jnp.einsum(
            "thr,sr->hts", q_rot[..., NOPE:], key_rot, preferred_element_type=jnp.float32
        )
        return jnp.where(allowed[None], dots * score_scale, -1000000000.0)

    scores = raw_scores()
    row_peak = jnp.max(scores, axis=-1, keepdims=True)
    log_total = jnp.log(jnp.sum(jnp.exp(scores - row_peak), axis=-1, keepdims=True)) + row_peak
    attn_probs = jnp.exp(scores - log_total)
    mixed_heads = (
        jnp.einsum(
            "hts,shv->thv",
            attn_probs.astype(jnp.bfloat16),
            values,
            preferred_element_type=jnp.float32,
        )
        .astype(jnp.bfloat16)
        .reshape(length, head_count * VDIM)
    )
    attn_out = lax.psum(
        jnp.dot(mixed_heads, output_full, preferred_element_type=jnp.float32).astype(jnp.bfloat16),
        "tensor",
    ).astype(jnp.float32)
    middle = residual_stream + attn_out
    inv_two = norm_scale(middle)
    hat_two = middle * inv_two
    feedforward_normed_input = (hat_two * feedforward_norm_scale).astype(jnp.bfloat16)
    shared_gate_act = jnp.dot(
        feedforward_normed_input, gate_full, preferred_element_type=jnp.float32
    )
    shared_up_act = jnp.dot(feedforward_normed_input, lift_full, preferred_element_type=jnp.float32)
    shared_hidden = (jax.nn.silu(shared_gate_act) * shared_up_act).astype(jnp.bfloat16)
    shared_out = jnp.dot(shared_hidden, lower_full, preferred_element_type=jnp.float32)
    flat_ids = expert_ids.reshape(-1)
    member = (flat_ids[:, None] == jnp.arange(experts_all, dtype=jnp.int32)[None, :]).astype(
        jnp.int32
    )
    slot_rank = jnp.sum((jnp.cumsum(member, axis=0) - member) * member, axis=1)
    slot_index = flat_ids * capacity + slot_rank
    flat_weight = route_weight.reshape(-1)
    send_rows = (
        jnp.zeros((experts_all * capacity, model_width), jnp.bfloat16)
        .at[slot_index]
        .set(jnp.repeat(feedforward_normed_input, choose, axis=0))
    )
    received_rows = to_experts(send_rows, rank_count, local_experts, capacity)
    expert_gate_activation = jnp.einsum(
        "secd,edf->secf", received_rows, expert_gate, preferred_element_type=jnp.float32
    )
    expert_up_activation = jnp.einsum(
        "secd,edf->secf", received_rows, expert_up_projection, preferred_element_type=jnp.float32
    )
    expert_hidden = (jax.nn.silu(expert_gate_activation) * expert_up_activation).astype(
        jnp.bfloat16
    )
    expert_out = jnp.einsum(
        "secf,efd->secd", expert_hidden, expert_down, preferred_element_type=jnp.float32
    ).astype(jnp.bfloat16)
    back_rows, per_expert, row_start = from_experts(expert_out, capacity)
    routed = pick_rows(
        back_rows, flat_ids, slot_rank, per_expert, row_start, flat_weight, length, choose
    )
    block_out = lax.psum((shared_out + routed).astype(jnp.bfloat16), "tensor").astype(jnp.float32)
    output = (middle + block_out).astype(jnp.bfloat16)
    grad_out = cotangent.astype(jnp.float32)
    grad_pairs = (jnp.repeat(grad_out, choose, axis=0) * flat_weight[:, None]).astype(jnp.bfloat16)
    grad_send = (
        jnp.zeros((experts_all * capacity, model_width), jnp.bfloat16)
        .at[slot_index]
        .set(grad_pairs)
    )
    grad_arrived = to_experts(grad_send, rank_count, local_experts, capacity)
    hidden_state_gradient = jnp.einsum(
        "secd,efd->secf", grad_arrived, expert_down, preferred_element_type=jnp.float32
    )
    grad_expert_down = jnp.einsum(
        "secf,secd->efd", expert_hidden, grad_arrived, preferred_element_type=jnp.float32
    )
    expert_gate_gradient, expert_up_gradient = swish_derivative(
        hidden_state_gradient, expert_gate_activation, expert_up_activation
    )
    expert_gate_gradient = expert_gate_gradient.astype(jnp.bfloat16)
    expert_up_gradient = expert_up_gradient.astype(jnp.bfloat16)
    grad_expert_gate = jnp.einsum(
        "zxmi,zxmh->xih", received_rows, expert_gate_gradient, preferred_element_type=jnp.float32
    )
    grad_expert_up = jnp.einsum(
        "zxmi,zxmh->xih", received_rows, expert_up_gradient, preferred_element_type=jnp.float32
    )
    grad_inputs = jnp.einsum(
        "azlh,zoh->azlo", expert_gate_gradient, expert_gate, preferred_element_type=jnp.float32
    )
    grad_inputs = (
        grad_inputs
        + jnp.einsum(
            "azlh,zoh->azlo",
            expert_up_gradient,
            expert_up_projection,
            preferred_element_type=jnp.float32,
        )
    ).astype(jnp.bfloat16)
    grad_back, per_back, start_back = from_experts(grad_inputs, capacity)
    routed_grad = pick_rows(
        grad_back,
        flat_ids,
        slot_rank,
        per_back,
        start_back,
        jnp.ones_like(flat_weight),
        length,
        choose,
    )
    grad_shared_hidden = dot_last(cotangent, lower_full)
    grad_sgate, grad_sup = swish_derivative(grad_shared_hidden, shared_gate_act, shared_up_act)
    grad_sgate = grad_sgate.astype(jnp.bfloat16)
    grad_sup = grad_sup.astype(jnp.bfloat16)
    grad_lower = dot_first(shared_hidden, cotangent)
    grad_gate_full = dot_first(feedforward_normed_input, grad_sgate)
    grad_lift_full = dot_first(feedforward_normed_input, grad_sup)
    grad_normed_two = dot_last(grad_sgate, gate_full) + dot_last(grad_sup, lift_full) + routed_grad
    grad_normed_two = lax.psum(grad_normed_two.astype(jnp.bfloat16), "tensor").astype(jnp.float32)
    token_share = length // groups
    share_start = lax.axis_index("tensor") * token_share
    grad_gain_two = jnp.sum(
        lax.dynamic_slice_in_dim(grad_normed_two * hat_two, share_start, token_share, 0), axis=0
    )
    grad_middle = grad_out + norm_back(grad_normed_two * feedforward_norm_scale, hat_two, inv_two)
    grad_middle_low = grad_middle.astype(jnp.bfloat16)
    grad_output_full = dot_first(mixed_heads, grad_middle_low)
    grad_mixed = (
        dot_last(grad_middle_low, output_full)
        .astype(jnp.bfloat16)
        .reshape(length, head_count, VDIM)
    )
    scores = raw_scores()
    attn_probs = jnp.exp(scores - log_total)
    grad_probs = jnp.einsum("thv,shv->hts", grad_mixed, values, preferred_element_type=jnp.float32)
    grad_values = jnp.einsum(
        "hts,thv->shv",
        attn_probs.astype(jnp.bfloat16),
        grad_mixed,
        preferred_element_type=jnp.float32,
    )
    row_delta = jnp.sum(attn_probs * grad_probs, axis=-1, keepdims=True)
    grad_scores = (attn_probs * (grad_probs - row_delta)).astype(jnp.bfloat16)
    grad_q_nope = (
        jnp.einsum("hts,shd->thd", grad_scores, key_nope, preferred_element_type=jnp.float32)
        * score_scale
    )
    grad_q_rope = (
        jnp.einsum("hts,sr->thr", grad_scores, key_rot, preferred_element_type=jnp.float32)
        * score_scale
    )
    grad_k_nope = (
        jnp.einsum(
            "hts,thd->shd", grad_scores, q_rot[..., :NOPE], preferred_element_type=jnp.float32
        )
        * score_scale
    )
    grad_k_rope = (
        jnp.einsum(
            "hts,thr->sr", grad_scores, q_rot[..., NOPE:], preferred_element_type=jnp.float32
        )
        * score_scale
    )
    grad_queries = jnp.concatenate(
        [grad_q_nope, rotate(grad_q_rope, cosine[:, None, :], -sine_part[:, None, :])], axis=-1
    )
    grad_queries = grad_queries.astype(jnp.bfloat16).reshape(length, head_count * (NOPE + ROPE))
    grad_keyval = (
        jnp.concatenate([grad_k_nope, grad_values], axis=-1)
        .astype(jnp.bfloat16)
        .reshape(length, head_count * (NOPE + VDIM))
    )
    grad_query_full = dot_first(normed_one, grad_queries)
    grad_expand_full = dot_first(latent_low, grad_keyval)
    grad_latent = dot_last(grad_keyval, expand_full)
    grad_gain_kv = jnp.sum(grad_latent * hat_kv, axis=0)
    grad_latent_raw = norm_back(grad_latent * latent_norm_scale, hat_kv, inv_kv)
    grad_compressed = jnp.concatenate(
        [grad_latent_raw, rotate(grad_k_rope, cosine, -sine_part)], axis=-1
    ).astype(jnp.bfloat16)
    grad_latent_full = dot_first(normed_one, grad_compressed)
    grad_normed_one = dot_last(grad_queries, query_full) + dot_last(grad_compressed, latent_full)
    grad_normed_one = lax.psum(grad_normed_one.astype(jnp.bfloat16), "tensor").astype(jnp.float32)
    grad_gain_one = jnp.sum(
        lax.dynamic_slice_in_dim(grad_normed_one * hat_one, share_start, token_share, 0), axis=0
    )
    grad_tokens = grad_middle + norm_back(grad_normed_one * attention_norm_scale, hat_one, inv_one)
    (
        grad_q_weight,
        grad_kvb_weight,
        grad_out_weight,
        grad_shared_gate,
        grad_shared_up,
        grad_shared_down,
    ) = (
        lax.psum_scatter(
            grad_query_full.astype(jnp.bfloat16), "dp", scatter_dimension=0, tiled=True
        ).astype(jnp.float32),
        lax.psum_scatter(
            grad_expand_full.astype(jnp.bfloat16), "dp", scatter_dimension=0, tiled=True
        ).astype(jnp.float32),
        lax.psum_scatter(
            grad_output_full.astype(jnp.bfloat16), "dp", scatter_dimension=1, tiled=True
        ).astype(jnp.float32),
        lax.psum_scatter(
            grad_gate_full.astype(jnp.bfloat16), "dp", scatter_dimension=0, tiled=True
        ).astype(jnp.float32),
        lax.psum_scatter(
            grad_lift_full.astype(jnp.bfloat16), "dp", scatter_dimension=0, tiled=True
        ).astype(jnp.float32),
        lax.psum_scatter(
            grad_lower.astype(jnp.bfloat16), "dp", scatter_dimension=1, tiled=True
        ).astype(jnp.float32),
    )
    grad_kva_weight, grad_norm1_gain, grad_kv_gain, grad_norm2_gain = (
        lax.psum_scatter(grad_latent_full, ("dp", "tensor"), scatter_dimension=0, tiled=True),
        lax.psum_scatter(grad_gain_one, ("dp", "tensor"), scatter_dimension=0, tiled=True),
        lax.psum_scatter(grad_gain_kv, ("dp", "tensor"), scatter_dimension=0, tiled=True),
        lax.psum_scatter(grad_gain_two, ("dp", "tensor"), scatter_dimension=0, tiled=True),
    )
    return (
        output,
        grad_tokens,
        grad_norm1_gain,
        grad_q_weight,
        grad_kva_weight,
        grad_kv_gain,
        grad_kvb_weight,
        grad_out_weight,
        grad_norm2_gain,
        grad_shared_gate,
        grad_shared_up,
        grad_shared_down,
        grad_expert_gate,
        grad_expert_up,
        grad_expert_down,
    )


def solution(mesh):
    in_specs = (
        P("dp", None),
        P("dp", None),
        P("dp", None),
        P("dp", None),
        P(("dp", "tensor")),
        P("dp", "tensor"),
        P(("dp", "tensor"), None),
        P(("dp", "tensor")),
        P("dp", "tensor"),
        P("tensor", "dp"),
        P(("dp", "tensor")),
        P("dp", "tensor"),
        P("dp", "tensor"),
        P("tensor", "dp"),
        P("dp", None, "tensor"),
        P("dp", None, "tensor"),
        P("dp", "tensor", None),
        P("dp", None),
    )
    out_specs = (
        P("dp", None),
        P("dp", None),
        P(("dp", "tensor")),
        P("dp", "tensor"),
        P(("dp", "tensor"), None),
        P(("dp", "tensor")),
        P("dp", "tensor"),
        P("tensor", "dp"),
        P(("dp", "tensor")),
        P("dp", "tensor"),
        P("dp", "tensor"),
        P("tensor", "dp"),
        P("dp", None, "tensor"),
        P("dp", None, "tensor"),
        P("dp", "tensor", None),
    )
    return jax.shard_map(local, mesh=mesh, in_specs=in_specs, out_specs=out_specs, check_vma=False)
```

profile of v0, /device:TPU:0, one launch (start us, length us, event | category | flops | bytes accessed | tf_op | source)
XLA Modules:
  0.0 2629.5 jit_solution(13420716831015691509)
XLA Ops:
  17.0 42.2 %all-reduce.7 = (bf16[2048]{0:T(1024)(128)(2,1)S(1)}, bf16[512]{0:T(512)(128)(2,1)S(1)}, bf16[2048]{0:T(1024)(128)(2,1)}) all-reduce(bf16[2048]{0:T(1024)(128)(2,1)S(1)} %dynamic-update-slice, bf16[512]{0:T(512)(128)(2,1)S(1)} %dynamic-update-slice.1, ...), channel_id=1, replica_groups=mesh['dp'=8,'tensor'=4] {'dp','tensor'}, use_global_device_ids=true, to_apply=%add | all-reduce | flops 4608 | bytes 18432
  60.2 11.2 all-gather.8.cloned.1.call-done
  76.2 18.1 all-gather.10.cloned.1.call-done
  106.3 27.5 %all-gather.12.cloned.1.call-done = bf16[2048,768]{1,0:T(8,128)(2,1)} async-done(((bf16[256,768]{1,0:T(8,128)(2,1)}), bf16[2048,768]{1,0:T(8,128)(2,1)}) %all-gather.12.cloned.1.call-update) | async-done | bytes 3145744 | tf_op jit(solution)/shard_map/all_gather | solution.py:140
  143.3 21.5 all-gather.14.cloned.1.call-done
  170.0 9.6 reduce-window.19
  181.2 56.6 %all-reduce.13.cloned.1.call-done = bf16[512,2048]{1,0:T(8,128)(2,1)} async-done(((bf16[512,2048]{1,0:T(8,128)(2,1)}), bf16[512,2048]{1,0:T(8,128)(2,1)}) %all-reduce.13.cloned.1.call-update) | async-done | bytes 2097168 | tf_op jit(solution)/shard_map/psum | solution.py:213
  244.8 7.4 broadcast_in_dim.43
  252.2 20.6 reshape.429
  272.8 29.2 %scatter_custom_fusion = bf16[4608,2048]{1,0:T(8,128)(2,1)} fusion(s32[3072]{0:T(1024)S(1)} %bitcast.210, bf16[3072,2048]{1,0:T(8,128)(2,1)} %reshape.429, bf16[]{:T(256)} %constant.17.clone.1), kind=kCustom, calls=%fused_computation.20 | custom fusion | bytes 18874880 | tf_op jit(solution)/shard_map/scatter | solution.py:237
  302.0 6.1 all-to-all-start
  308.1 11.4 broadcast_in_dim.45
  319.5 29.6 %reshape.401 = f32[3072,2048]{1,0:T(8,128)} reshape(f32[512,6,2048]{2,1,0:T(8,128)} %broadcast_in_dim.45) | data formatting | bytes 50331648 | tf_op jit(solution)/shard_map/reshape | solution.py:259
  349.4 10.0 mul.424
  359.4 33.4 %scatter_custom_fusion.1 = bf16[4608,2048]{1,0:T(8,128)(2,1)} fusion(s32[3072]{0:T(1024)S(1)} %bitcast.211, f32[3072,2048]{1,0:T(8,128)} %reshape.401, f32[3072,2048]{1,0:T(8,128)} %mul.424, bf16[]{:T(256)} %constant.17.clone.1), kind=kCustom, calls=%fused_computation.18 | custom fusion | flops 12582912 | bytes 69206016 | tf_op jit(solution)/shard_map/scatter | solution.py:263
  392.8 323.9 %all-to-all-done = bf16[8,576,2048]{2,1,0:T(8,128)(2,1)} async-done(((bf16[8,576,2048]{2,1,0:T(8,128)(2,1)}), bf16[8,576,2048]{2,1,0:T(8,128)(2,1)}, u32[]{:S(2)}, u32[]{:S(2)}) %all-to-all-start) | async-done | bytes 18874400 | tf_op jit(solution)/shard_map/all_to_all | solution.py:77
  716.7 5.9 all-to-all-start.2
  722.6 17.2 fusion.7
  739.8 17.2 fusion.5
  756.9 374.2 %all-to-all-done.2 = bf16[8,576,2048]{2,1,0:T(8,128)(2,1)} async-done(((bf16[8,576,2048]{2,1,0:T(8,128)(2,1)}), bf16[8,576,2048]{2,1,0:T(8,128)(2,1)}, u32[]{:S(2)}, u32[]{:S(2)}) %all-to-all-start.2) | async-done | bytes 18874400 | tf_op jit(solution)/shard_map/all_to_all | solution.py:77
  1131.1 20.2 fusion.17
  1151.4 19.9 fusion.25
  1171.3 25.7 fusion
  1197.0 16.9 copy.153
  1213.9 6.2 all-to-all-start.3
  1220.1 15.8 convert_bitcast_fusion
  1235.9 17.0 copy.149
  1252.9 375.8 %all-to-all-done.3 = bf16[8,576,2048]{2,1,0:T(8,128)(2,1)} async-done(((bf16[8,576,2048]{2,1,0:T(8,128)(2,1)}), bf16[8,576,2048]{2,1,0:T(8,128)(2,1)}, u32[]{:S(2)}, u32[]{:S(2)}) %all-to-all-start.3) | async-done | bytes 18874400 | tf_op jit(solution)/shard_map/all_to_all | solution.py:89
  1628.7 6.1 all-to-all-start.1
  1637.5 82.7 %all-gather.16.cloned.1.call-done = bf16[2048,704]{0,1:T(8,128)(2,1)} async-done(((bf16[256,704]{0,1:T(8,128)(2,1)}), bf16[2048,704]{0,1:T(8,128)(2,1)}) %all-gather.16.cloned.1.call-update) | async-done | bytes 2883600 | tf_op jit(solution)/shard_map/all_gather | solution.py:143
  1724.8 89.3 %all-gather.18.cloned.1.call-done = bf16[2048,704]{0,1:T(8,128)(2,1)} async-done(((bf16[256,704]{0,1:T(8,128)(2,1)}), bf16[2048,704]{0,1:T(8,128)(2,1)}) %all-gather.18.cloned.1.call-update) | async-done | bytes 2883600 | tf_op jit(solution)/shard_map/all_gather | solution.py:144
  1819.3 66.9 %all-gather.20.cloned.1.call-done = bf16[704,2048]{1,0:T(8,128)(2,1)} async-done(((bf16[704,256]{1,0:T(8,128)(2,1)}), bf16[704,2048]{1,0:T(8,128)(2,1)}) %all-gather.20.cloned.1.call-update) | async-done | bytes 2883600 | tf_op jit(solution)/shard_map/all_gather | solution.py:145
  1886.3 6.1 multiply_convert_fusion.5
  1896.3 33.0 %gather_fusion.1 = bf16[3072,2048]{1,0:T(8,128)(2,1)} fusion(bf16[4608,2048]{1,0:T(8,128)(2,1)} %bitcast.35, s32[3072]{0:T(1024)S(1)} %broadcast_clamp_fusion), kind=kCustom, calls=%fused_computation.1 | custom fusion | bytes 25178112 | tf_op jit(solution)/shard_map/gather | solution.py:104
  1929.3 22.1 reshape.408
  1951.4 17.9 multiply_reduce_fusion
  1986.2 179.1 %all-to-all-done.1 = bf16[8,576,2048]{2,1,0:T(8,128)(2,1)} async-done(((bf16[8,576,2048]{2,1,0:T(8,128)(2,1)}), bf16[8,576,2048]{2,1,0:T(8,128)(2,1)}, u32[]{:S(2)}, u32[]{:S(2)}) %all-to-all-start.1) | async-done | bytes 18874400 | tf_op jit(solution)/shard_map/all_to_all | solution.py:89
  2165.3 32.8 %gather_fusion = bf16[3072,2048]{1,0:T(8,128)(2,1)} fusion(bf16[4608,2048]{1,0:T(8,128)(2,1)} %bitcast.25, s32[3072]{0:T(1024)S(1)} %broadcast_clamp_fusion), kind=kCustom, calls=%fused_computation | custom fusion | bytes 25178112 | tf_op jit(solution)/shard_map/gather | solution.py:104
  2198.1 22.2 reshape.407
  2220.3 17.4 multiply_reduce_fusion.1
  2287.9 15.6 convolution_bitcast_fusion.1
  2303.5 15.6 convolution_bitcast_fusion
  2319.1 15.4 fusion.30
  2339.8 56.3 %all-reduce.17.cloned.1.call-done = (bf16[512,2048]{1,0:T(8,128)(2,1)}, bf16[512,2048]{1,0:T(8,128)(2,1)}) async-done(((bf16[512,2048]{1,0:T(8,128)(2,1)}, bf16[512,2048]{1,0:T(8,128)(2,1)}), (bf16[512,2048]{1,0:T(8,128)(2,1)}, bf16[512,2048]{1,0:T(8,128)(2,1)})) %all-reduce.17.cloned.1.call-update) | async-done | bytes 4194320 | tf_op jit(solution)/shard_map/psum | solution.py:256
  2403.3 40.1 %all-reduce.6 = (f32[2048]{0:T(1024)S(1)}, f32[512]{0:T(512)S(1)}, f32[2048]{0:T(1024)S(1)}) all-reduce(f32[2048]{0:T(1024)S(1)} %fusion.48, f32[512]{0:T(512)S(1)} %get-tuple-element.15, f32[2048]{0:T(1024)S(1)} %fusion.47), channel_id=2, replica_groups=mesh['dp'=8,'tensor'=4] {'dp','tensor'}, use_global_device_ids=true, to_apply=%region_24.25.clone | all-reduce | flops 4608 | bytes 36864
  2446.9 6.2 multiply_add_fusion
  2453.1 22.5 reduce-scatter.8.cloned.1.call-done
  2477.5 145.3 %reduce-scatter.10.cloned.1.call-done = f32[64,576]{1,0:T(8,128)} async-done(((f32[2048,576]{1,0:T(8,128)}), f32[64,576]{1,0:T(8,128)}) %reduce-scatter.10.cloned.1.call-update) | async-done | bytes 147472 | tf_op jit(solution)/shard_map/reduce_scatter | solution.py:411
  (297 shorter events, 151.3 us)
Async XLA Ops:
  7.2 64.3 %all-gather.8.cloned.1.call-start = ((), (), s32[]{:S(2)}) async-start(), calls=%async_computation.11 | async-start | bytes 2703360 | tf_op jit(solution)/shard_map/all_gather | solution.py:148
  7.9 86.4 %all-gather.10.cloned.1.call-start = ((), (), s32[]{:S(2)}) async-start(), calls=%async_computation.12 | async-start | bytes 1179648 | tf_op jit(solution)/shard_map/all_gather | solution.py:141
  8.7 125.2 %all-gather.12.cloned.1.call-start = ((), (), s32[]{:S(2)}) async-start(), calls=%async_computation.13 | async-start | bytes 3538944 | tf_op jit(solution)/shard_map/all_gather | solution.py:140
  9.4 155.5 %all-gather.14.cloned.1.call-start = ((), (), s32[]{:S(2)}) async-start(), calls=%async_computation.14 | async-start | bytes 2359296 | tf_op jit(solution)/shard_map/all_gather | solution.py:142
  10.0 227.8 %all-reduce.13.cloned.1.call-start = ((), (), s32[]{:S(2)}) async-start(), calls=%async_computation.15 | async-start | bytes 4194304 | tf_op jit(solution)/shard_map/psum | solution.py:213
  14.4 60.9 %copy-start.64 = (f32[512]{0:T(512)}, f32[512]{0:T(512)S(1)}, u32[]{:S(2)}) copy-start(f32[512]{0:T(512)S(1)} %add_rsqrt_fusion.2) | copy-start | bytes 6148
  59.2 74.7 %copy-start.53 = (f32[2048]{0:T(1024)}, f32[2048]{0:T(1024)S(1)}, u32[]{:S(2)}) copy-start(f32[2048]{0:T(1024)S(1)} %convert_element_type.187) | copy-start | bytes 24580
  59.2 35.1 %copy-start.61 = (f32[512]{0:T(512)}, f32[512]{0:T(512)S(1)}, u32[]{:S(2)}) copy-start(f32[512]{0:T(512)S(1)} %convert_element_type.189) | copy-start | bytes 6148
  60.2 44.5 %copy-start.57 = (f32[512]{0:T(512)}, f32[512]{0:T(512)S(1)}, u32[]{:S(2)}) copy-start(f32[512]{0:T(512)S(1)} %subtract_convert_fusion.2) | copy-start | bytes 6148
  75.3 29.3 %copy-start.10 = (f32[512,576]{0,1:T(8,128)}, f32[512,576]{0,1:T(8,128)S(1)}, u32[]{:S(2)}) copy-start(f32[512,576]{0,1:T(8,128)S(1)} %fusion.83) | copy-start | bytes 3538948
  76.2 57.6 %copy-start.2 = (bf16[512,2048]{1,0:T(8,128)(2,1)S(1)}, bf16[512,2048]{1,0:T(8,128)(2,1)}, u32[]{:S(2)}) copy-start(bf16[512,2048]{1,0:T(8,128)(2,1)} %param.18) | copy-start | bytes 6291460
  106.3 31.4 %copy-start.36 = (f32[512,32]{0,1:T(8,128)S(1)}, f32[512,32]{0,1:T(8,128)}, u32[]{:S(2)}) copy-start(f32[512,32]{0,1:T(8,128)} %get-tuple-element.52) | copy-start | bytes 196612
  106.3 31.4 %copy-start.46 = (f32[512,32]{0,1:T(8,128)S(1)}, f32[512,32]{0,1:T(8,128)}, u32[]{:S(2)}) copy-start(f32[512,32]{0,1:T(8,128)} %get-tuple-element.51) | copy-start | bytes 196612
  106.3 31.5 %copy-start.18 = (bf16[512,4,128]{2,1,0:T(4,128)(2,1)S(1)}, bf16[512,4,128]{2,1,0:T(4,128)(2,1)}, u32[]{:S(2)}) copy-start(bf16[512,4,128]{2,1,0:T(4,128)(2,1)} %get-tuple-element.40) | copy-start | bytes 1572868
  143.3 25.7 copy-start.38
  143.3 25.8 copy-start.55
  169.0 11.2 copy-start.67
  180.2 63.3 %copy-start.49 = (f32[2048]{0:T(1024)}, f32[2048]{0:T(1024)S(1)}, u32[]{:S(2)}) copy-start(f32[2048]{0:T(1024)S(1)} %convert_element_type.199) | copy-start | bytes 24580
  180.5 63.0 %copy-start.51 = (s32[3072]{0:T(1024)}, s32[3072]{0:T(1024)S(1)}, u32[]{:S(2)}) copy-start(s32[3072]{0:T(1024)S(1)} %fusion.59) | copy-start | bytes 36868
  302.0 414.6 %all-to-all-start = ((bf16[8,576,2048]{2,1,0:T(8,128)(2,1)}), bf16[8,576,2048]{2,1,0:T(8,128)(2,1)}, u32[]{:S(2)}, u32[]{:S(2)}) async-start(bf16[8,576,2048]{2,1,0:T(8,128)(2,1)} %bitcast.189), calls=%async_computation | async-start | bytes 37748736 | tf_op jit(solution)/shard_map/all_to_all | solution.py:77
  319.5 29.6 %copy-start.66 = (f32[512,6]{0,1:T(8,128)S(1)}, f32[512,6]{0,1:T(8,128)}, u32[]{:S(2)}) copy-start(f32[512,6]{0,1:T(8,128)} %param.21) | copy-start | bytes 36868
  349.2 10.2 copy-start.25
  716.7 414.5 %all-to-all-start.2 = ((bf16[8,576,2048]{2,1,0:T(8,128)(2,1)}), bf16[8,576,2048]{2,1,0:T(8,128)(2,1)}, u32[]{:S(2)}, u32[]{:S(2)}) async-start(bf16[8,576,2048]{2,1,0:T(8,128)(2,1)} %bitcast.187), calls=%async_computation.2 | async-start | bytes 37748736 | tf_op jit(solution)/shard_map/all_to_all | solution.py:77
  1151.4 19.9 copy-start.23
  1213.9 6.2 copy-start.76
  1213.9 414.8 %all-to-all-start.3 = ((bf16[8,576,2048]{2,1,0:T(8,128)(2,1)}), bf16[8,576,2048]{2,1,0:T(8,128)(2,1)}, u32[]{:S(2)}, u32[]{:S(2)}) async-start(bf16[8,576,2048]{2,1,0:T(8,128)(2,1)} %bitcast.190), calls=%async_computation.3 | async-start | bytes 37748736 | tf_op jit(solution)/shard_map/all_to_all | solution.py:89
  1628.7 8.4 copy-start.52
  1628.7 8.7 copy-start.56
  1628.7 8.7 copy-start.26
  1628.7 91.5 %copy-start.15 = (bf16[512,2048]{1,0:T(8,128)(2,1)S(1)}, bf16[512,2048]{1,0:T(8,128)(2,1)}, u32[]{:S(2)}) copy-start(bf16[512,2048]{1,0:T(8,128)(2,1)} %copy-done.14) | copy-start | bytes 6291460
  1628.7 536.6 %all-to-all-start.1 = ((bf16[8,576,2048]{2,1,0:T(8,128)(2,1)}), bf16[8,576,2048]{2,1,0:T(8,128)(2,1)}, u32[]{:S(2)}, u32[]{:S(2)}) async-start(bf16[8,576,2048]{2,1,0:T(8,128)(2,1)} %bitcast.188), calls=%async_computation.1 | async-start | bytes 37748736 | tf_op jit(solution)/shard_map/all_to_all | solution.py:89
  1634.8 85.4 %all-gather.16.cloned.1.call-start = ((), (), s32[]{:S(2)}) async-start(), calls=%async_computation.16 | async-start | bytes 3244032 | tf_op jit(solution)/shard_map/all_gather | solution.py:143
  1635.3 178.7 %all-gather.18.cloned.1.call-start = ((), (), s32[]{:S(2)}) async-start(), calls=%async_computation.17 | async-start | bytes 3244032 | tf_op jit(solution)/shard_map/all_gather | solution.py:144
  1636.1 250.2 %all-gather.20.cloned.1.call-start = ((), (), s32[]{:S(2)}) async-start(), calls=%async_computation.18 | async-start | bytes 3244032 | tf_op jit(solution)/shard_map/all_gather | solution.py:145
  1636.8 604.2 %all-reduce.15.cloned.1.call-start = ((), (), s32[]{:S(2)}) async-start(), calls=%async_computation.19 | async-start | bytes 4194304 | tf_op jit(solution)/shard_map/psum | solution.py:314
  1724.8 161.5 %copy-start.13 = (bf16[512,2048]{1,0:T(8,128)(2,1)S(1)}, bf16[512,2048]{1,0:T(8,128)(2,1)}, u32[]{:S(2)}) copy-start(bf16[512,2048]{1,0:T(8,128)(2,1)} %param.35) | copy-start | bytes 6291460
  1951.4 17.9 copy-start.22
  1951.4 17.9 copy-start.71
  1951.4 17.9 copy-start.74
  1972.8 309.4 %reduce-scatter.16.cloned.1.call-start = ((), (), s32[]{:S(2)}) async-start(), calls=%async_computation.24 | async-start | bytes 3244032 | tf_op jit(solution)/shard_map/reduce_scatter | solution.py:400
  1977.7 306.4 %reduce-scatter.18.cloned.1.call-start = ((), (), s32[]{:S(2)}) async-start(), calls=%async_computation.25 | async-start | bytes 3244032 | tf_op jit(solution)/shard_map/reduce_scatter | solution.py:403
  1982.9 303.1 %reduce-scatter.20.cloned.1.call-start = ((), (), s32[]{:S(2)}) async-start(), calls=%async_computation.26 | async-start | bytes 3244032 | tf_op jit(solution)/shard_map/reduce_scatter | solution.py:406
  1986.2 351.9 %reduce-scatter.12.cloned.1.call-start = ((), (), s32[]{:S(2)}) async-start(), calls=%async_computation.22 | async-start | bytes 1179648 | tf_op jit(solution)/shard_map/reduce_scatter | solution.py:394
  2220.3 17.4 copy-start.70
  2259.5 136.5 %all-reduce.17.cloned.1.call-start = ((), (), s32[]{:S(2)}) async-start(), calls=%async_computation.27 | async-start | bytes 8388608 | tf_op jit(solution)/shard_map/psum | solution.py:256
  2267.9 177.3 %reduce-scatter.14.cloned.1.call-start = ((), (), s32[]{:S(2)}) async-start(), calls=%async_computation.23 | async-start | bytes 2359296 | tf_op jit(solution)/shard_map/reduce_scatter | solution.py:397
  2273.8 201.8 %reduce-scatter.8.cloned.1.call-start = ((), (), s32[]{:S(2)}) async-start(), calls=%async_computation.20 | async-start | bytes 3538944 | tf_op jit(solution)/shard_map/reduce_scatter | solution.py:391
  2277.7 345.1 %reduce-scatter.10.cloned.1.call-start = ((), (), s32[]{:S(2)}) async-start(), calls=%async_computation.21 | async-start | bytes 5406720 | tf_op jit(solution)/shard_map/reduce_scatter | solution.py:411
  (50 other events, 149.6 us)
Sparse Core Ops, SparseCore 0:
  10.9 60.5 all-gather.7
  73.0 21.2 all-gather.9
  96.0 37.8 all-gather.11
  135.3 29.5 all-gather.13
  169.2 68.5 all-reduce.12
  1636.8 83.2 all-gather.15
  1721.8 92.2 all-gather.17
  1815.7 70.5 all-gather.19
  1972.9 67.0 all-reduce.14
  2042.7 52.4 reduce-scatter.15
  2097.6 69.0 reduce-scatter.17
  2168.8 38.5 reduce-scatter.19
  2259.6 30.4 reduce-scatter.11
  2294.1 101.9 all-reduce.16
  2398.2 36.3 reduce-scatter.13
  2436.7 38.7 reduce-scatter.7
  2478.3 144.4 reduce-scatter.9
where the time goes:
time: 2640 us; the launch traced here: 2630 us
  waiting for transfers between devices  1860 us (70%)
  local copies, waits for them, and re-layouts  276 us (10%)
  matrix products  248 us (9%)
  other arithmetic  127 us (5%)
  blocking collectives  82.3 us (3%)
    all_to_all x2, waiting for transfers between devices, to_experts(): lax.all_to_all(buffer.reshape(rank_count, local_experts * capacity, model...  698 us
    all_to_all x2, waiting for transfers between devices, from_experts(): lax.all_to_all(partial_value.reshape(rank_count, local_experts * capacity...  555 us
    reduce_scatter x1, waiting for transfers between devices, local(): lax.psum_scatter(grad_latent_full, ('dp', 'tensor'), scatter_dimension=0,...  145 us
    all_gather x1, waiting for transfers between devices, local(): lax.all_gather(shared_up, 'dp', axis=0, tiled=True)  89.3 us
    all_gather x1, waiting for transfers between devices, local(): lax.all_gather(shared_gate, 'dp', axis=0, tiled=True)  82.7 us
    unnamed x2, blocking collectives  82.3 us
    all_gather x1, waiting for transfers between devices, local(): lax.all_gather(shared_down, 'dp', axis=1, tiled=True)  66.9 us
    gather x2, local copies, waits for them, and re-layouts, pick_rows(): row_block[row_index].astype(jnp.float32)  65.8 us
  transfers between devices with their start and end apart: 21, of which 15 were waited for; matrix products, arithmetic and copies ran while one was open for 19% of the time, Pallas kernels for 0%

commit v1 on v0

--- a/solution.py
+++ b/solution.py
@@ -72,38 +72,23 @@
     )
 
 
-def to_experts(buffer, rank_count, local_experts, capacity):
-    model_width = buffer.shape[1]
-    moved = lax.all_to_all(
-        buffer.reshape(rank_count, local_experts * capacity, model_width),
-        "dp",
-        split_axis=0,
-        concat_axis=0,
-        tiled=True,
-    )
-    return moved.reshape(rank_count, local_experts, capacity, model_width)
-
-
-def from_experts(partial_value, capacity):
-    rank_count, local_experts, slot_count, model_width = partial_value.shape
-    moved = lax.all_to_all(
-        partial_value.reshape(rank_count, local_experts * capacity, model_width),
-        "dp",
-        split_axis=0,
-        concat_axis=0,
-        tiled=True,
-    )
-    return (moved.reshape(rank_count * local_experts * capacity, model_width), capacity, 0)
-
-
-def pick_rows(row_block, flat_ids, slot_rank, per_expert, row_start, pair_weight, length, choose):
-    local_rank = slot_rank - row_start
-    is_valid = (local_rank >= 0) & (local_rank < per_expert)
-    row_index = flat_ids * per_expert + jnp.clip(local_rank, 0, per_expert - 1)
-    picked = (
-        row_block[row_index].astype(jnp.float32) * jnp.where(is_valid, pair_weight, 0.0)[:, None]
-    )
-    return jnp.sum(picked.reshape(length, choose, row_block.shape[1]), axis=1)
+def slot_tables(ids_all, weights_all, first_expert, local_experts, capacity):
+    length = ids_all.shape[2]
+    experts = first_expert + jnp.arange(local_experts, dtype=jnp.int32)
+    named = ids_all[:, None] == experts[None, :, None, None]
+    member = jnp.any(named, axis=2)
+    pair_weight = jnp.sum(jnp.where(named, weights_all[:, None], 0.0), axis=2)
+    earlier = jnp.arange(length)[:, None] < jnp.arange(length)[None, :]
+    rank = jnp.einsum(
+        "set,tu->seu",
+        member.astype(jnp.bfloat16),
+        earlier.astype(jnp.bfloat16),
+        preferred_element_type=jnp.float32,
+    ).astype(jnp.int32)
+    slot = jnp.where(member, rank, -1)
+    chosen = slot[:, :, None, :] == jnp.arange(capacity, dtype=jnp.int32)[None, None, :, None]
+    slot_weight = jnp.sum(jnp.where(chosen, pair_weight[:, :, None, :], 0.0), axis=3)
+    return chosen.astype(jnp.bfloat16), slot_weight
 
 
 def local(
@@ -136,6 +121,14 @@
     capacity = groups * -(-(3 * length * choose) // (2 * experts_all * groups))
     head_count = q_weight.shape[1] // (NOPE + ROPE)
     score_scale = (NOPE + ROPE) ** (-0.5)
+    def quarter(rows):
+        share = rows.shape[0] // groups
+        return lax.dynamic_slice_in_dim(rows, lax.axis_index("tensor") * share, share, 0)
+
+    routing = jnp.concatenate([expert_ids.astype(jnp.float32).T, route_weight.T], axis=0)
+    routing_all = lax.all_gather(routing, "dp", axis=0, tiled=False)
+    ids_all, weights_all = routing_all[:, :choose], routing_all[:, choose:]
+    grad_all = lax.all_gather(quarter(cotangent), ("dp", "tensor"), axis=0, tiled=True)
     query_full, expand_full, output_full, gate_full, lift_full, lower_full = (
         lax.all_gather(q_weight, "dp", axis=0, tiled=True),
         lax.all_gather(kvb_weight, "dp", axis=0, tiled=True),
@@ -224,19 +217,24 @@
     shared_up_act = jnp.dot(feedforward_normed_input, lift_full, preferred_element_type=jnp.float32)
     shared_hidden = (jax.nn.silu(shared_gate_act) * shared_up_act).astype(jnp.bfloat16)
     shared_out = jnp.dot(shared_hidden, lower_full, preferred_element_type=jnp.float32)
-    flat_ids = expert_ids.reshape(-1)
-    member = (flat_ids[:, None] == jnp.arange(experts_all, dtype=jnp.int32)[None, :]).astype(
-        jnp.int32
-    )
-    slot_rank = jnp.sum((jnp.cumsum(member, axis=0) - member) * member, axis=1)
-    slot_index = flat_ids * capacity + slot_rank
-    flat_weight = route_weight.reshape(-1)
-    send_rows = (
-        jnp.zeros((experts_all * capacity, model_width), jnp.bfloat16)
-        .at[slot_index]
-        .set(jnp.repeat(feedforward_normed_input, choose, axis=0))
-    )
-    received_rows = to_experts(send_rows, rank_count, local_experts, capacity)
+    first_expert = lax.axis_index("dp") * local_experts
+    chosen, slot_weight = slot_tables(
+        ids_all.astype(jnp.int32), weights_all, first_expert, local_experts, capacity
+    )
+    rows_all = lax.all_gather(quarter(feedforward_normed_input), ("dp", "tensor"), axis=0, tiled=True)
+    received_rows = jnp.einsum(
+        "sect,std->secd",
+        chosen,
+        rows_all.reshape(rank_count, length, model_width),
+        preferred_element_type=jnp.float32,
+    ).astype(jnp.bfloat16)
+    grad_arrived = jnp.einsum(
+        "sect,std->secd",
+        chosen,
+        grad_all.reshape(rank_count, length, model_width),
+        preferred_element_type=jnp.float32,
+    )
+    grad_arrived = (grad_arrived * slot_weight[..., None]).astype(jnp.bfloat16)
     expert_gate_activation = jnp.einsum(
         "secd,edf->secf", received_rows, expert_gate, preferred_element_type=jnp.float32
     )
@@ -248,21 +246,17 @@
     )
     expert_out = jnp.einsum(
         "secf,efd->secd", expert_hidden, expert_down, preferred_element_type=jnp.float32
-    ).astype(jnp.bfloat16)
-    back_rows, per_expert, row_start = from_experts(expert_out, capacity)
-    routed = pick_rows(
-        back_rows, flat_ids, slot_rank, per_expert, row_start, flat_weight, length, choose
-    )
+    )
+    expert_out = (expert_out * slot_weight[..., None]).astype(jnp.bfloat16)
+    routed = jnp.einsum(
+        "sect,secd->std", chosen, expert_out, preferred_element_type=jnp.float32
+    ).astype(jnp.bfloat16)
+    routed = lax.psum_scatter(
+        routed.reshape(rank_count * length, model_width), "dp", scatter_dimension=0, tiled=True
+    ).astype(jnp.float32)
     block_out = lax.psum((shared_out + routed).astype(jnp.bfloat16), "tensor").astype(jnp.float32)
     output = (middle + block_out).astype(jnp.bfloat16)
     grad_out = cotangent.astype(jnp.float32)
-    grad_pairs = (jnp.repeat(grad_out, choose, axis=0) * flat_weight[:, None]).astype(jnp.bfloat16)
-    grad_send = (
-        jnp.zeros((experts_all * capacity, model_width), jnp.bfloat16)
-        .at[slot_index]
-        .set(grad_pairs)
-    )
-    grad_arrived = to_experts(grad_send, rank_count, local_experts, capacity)
     hidden_state_gradient = jnp.einsum(
         "secd,efd->secf", grad_arrived, expert_down, preferred_element_type=jnp.float32
     )
@@ -292,17 +286,12 @@
             preferred_element_type=jnp.float32,
         )
     ).astype(jnp.bfloat16)
-    grad_back, per_back, start_back = from_experts(grad_inputs, capacity)
-    routed_grad = pick_rows(
-        grad_back,
-        flat_ids,
-        slot_rank,
-        per_back,
-        start_back,
-        jnp.ones_like(flat_weight),
-        length,
-        choose,
-    )
+    routed_grad = jnp.einsum(
+        "sect,secd->std", chosen, grad_inputs, preferred_element_type=jnp.float32
+    ).astype(jnp.bfloat16)
+    routed_grad = lax.psum_scatter(
+        routed_grad.reshape(rank_count * length, model_width), "dp", scatter_dimension=0, tiled=True
+    ).astype(jnp.float32)
     grad_shared_hidden = dot_last(cotangent, lower_full)
     grad_sgate, grad_sup = swish_derivative(grad_shared_hidden, shared_gate_act, shared_up_act)
     grad_sgate = grad_sgate.astype(jnp.bfloat16)

time: 2640 us -> 1520 us (0.58)
  waiting for transfers between devices: 1860 us -> 996 us
  local copies, waits for them, and re-layouts: 276 us -> 26.5 us
  other arithmetic: 127 us -> 53.2 us
  matrix products: 248 us -> 316 us
    all_to_all x4 -> x0, waiting for transfers between devices: 1250 us -> none  [the longest x2 698 us: to_experts(): lax.all_to_all(buffer.reshape(rank_count, local_experts * capacity, model...]
    reduce_scatter x0 -> x2, waiting for transfers between devices: none -> 263 us  [the longest x1 148 us: local(): lax.psum_scatter(routed.reshape(rank_count * length, model_width), 'dp',...]
    all_gather x0 -> x2, waiting for transfers between devices: none -> 186 us  [the longest x1 97.3 us: local(): lax.all_gather(quarter(feedforward_normed_input), ('dp', 'tensor'), axis=...]
    all_gather x1, waiting for transfers between devices: 89.3 us -> 0.02 us  [local(): lax.all_gather(shared_up, 'dp', axis=0, tiled=True)]
    all_gather x1, waiting for transfers between devices: 82.7 us -> 0.01 us  [local(): lax.all_gather(shared_gate, 'dp', axis=0, tiled=True)]
    convert_element_type x4 -> x0, local copies, waits for them, and re-layouts: 78.2 us -> none  [the longest x2 44.3 us: pick_rows(): row_block[row_index].astype(jnp.float32)]
    all_gather x1, waiting for transfers between devices: 66.9 us -> 0.01 us  [local(): lax.all_gather(shared_down, 'dp', axis=1, tiled=True)]
    gather x2 -> x0, local copies, waits for them, and re-layouts: 65.8 us -> none  [pick_rows(): row_block[row_index].astype(jnp.float32)]
  transfers between devices with their start and end apart: 21 -> 21, of which waited for: 15 -> 16; matrix products, arithmetic and copies ran while one was open for 19% -> 25% of each run, Pallas kernels for 0% -> 0%
where the time goes in v1:
time: 1520 us; the launch traced here: 1510 us
  waiting for transfers between devices  996 us (66%)
  matrix products  316 us (21%)
  blocking collectives  98.2 us (6%)
  other arithmetic  53.2 us (4%)
  local copies, waits for them, and re-layouts  26.5 us (2%)
  between operations  15.5 us (1%)
    reduce_scatter x1, waiting for transfers between devices, local(): lax.psum_scatter(routed.reshape(rank_count * length, model_width), 'dp',...  148 us
    reduce_scatter x1, waiting for transfers between devices, local(): lax.psum_scatter(grad_latent_full, ('dp', 'tensor'), scatter_dimension=0,...  145 us
    reduce_scatter x1, waiting for transfers between devices, local(): lax.psum_scatter(routed_grad.reshape(rank_count * length, model_width), '...  115 us
    all_gather x1, waiting for transfers between devices, local(): lax.all_gather(quarter(feedforward_normed_input), ('dp', 'tensor'), axis=...  97.3 us
    all_gather x1, waiting for transfers between devices, local(): lax.all_gather(quarter(cotangent), ('dp', 'tensor'), axis=0, tiled=True)  89 us
    psum x1, waiting for transfers between devices, local(): lax.psum((shared_out + routed).astype(jnp.bfloat16), 'tensor')  86.5 us
    unnamed x2, blocking collectives  82.8 us
    psum x1, waiting for transfers between devices, local(): lax.psum(jnp.dot(mixed_heads, output_full, preferred_element_type=jnp.flo...  66.1 us
  transfers between devices with their start and end apart: 21, of which 16 were waited for; matrix products, arithmetic and copies ran while one was open for 25% of the time, Pallas kernels for 0%

profile of v1, /device:TPU:0, one launch (start us, length us, event | category | flops | bytes accessed | tf_op | source)
XLA Modules:
  0.0 1508.2 jit_solution(8672085634355310005)
XLA Ops:
  17.9 42.4 %all-reduce.7 = (bf16[2048]{0:T(1024)(128)(2,1)S(1)}, bf16[512]{0:T(512)(128)(2,1)S(1)}, bf16[2048]{0:T(1024)(128)(2,1)}) all-reduce(bf16[2048]{0:T(1024)(128)(2,1)S(1)} %dynamic-update-slice, bf16[512]{0:T(512)(128)(2,1)S(1)} %dynamic-update-slice.1, ...), channel_id=1, replica_groups=mesh['dp'=8,'tensor'=4] {'dp','tensor'}, use_global_device_ids=true, to_apply=%add | all-reduce | flops 4608 | bytes 18432
  60.4 11.3 all-gather.12.cloned.1.call-done
  71.7 3.9 fusion.104
  76.5 17.9 %all-gather.14.cloned.1.call-done = bf16[512,1024]{1,0:T(8,128)(2,1)} async-done(((bf16[64,1024]{1,0:T(8,128)(2,1)}), bf16[512,1024]{1,0:T(8,128)(2,1)}) %all-gather.14.cloned.1.call-update) | async-done | bytes 1048592 | tf_op jit(solution)/shard_map/all_gather | solution.py:134
  106.3 27.5 %all-gather.16.cloned.1.call-done = bf16[2048,768]{1,0:T(8,128)(2,1)} async-done(((bf16[256,768]{1,0:T(8,128)(2,1)}), bf16[2048,768]{1,0:T(8,128)(2,1)}) %all-gather.16.cloned.1.call-update) | async-done | bytes 3145744 | tf_op jit(solution)/shard_map/all_gather | solution.py:133
  133.9 3.8 fusion.103
  143.3 21.5 %all-gather.18.cloned.1.call-done = bf16[512,2048]{1,0:T(8,128)(2,1)} async-done(((bf16[512,256]{1,0:T(8,128)(2,1)}), bf16[512,2048]{1,0:T(8,128)(2,1)}) %all-gather.18.cloned.1.call-update) | async-done | bytes 2097168 | tf_op jit(solution)/shard_map/all_gather | solution.py:135
  164.9 4.2 convolution_convert_fusion.6
  171.6 66.1 %all-reduce.13.cloned.1.call-done = bf16[512,2048]{1,0:T(8,128)(2,1)} async-done(((bf16[512,2048]{1,0:T(8,128)(2,1)}), bf16[512,2048]{1,0:T(8,128)(2,1)}) %all-reduce.13.cloned.1.call-update) | async-done | bytes 2097168 | tf_op jit(solution)/shard_map/psum | solution.py:206
  247.8 15.4 %all-gather.1 = f32[8,12,512]{2,1,0:T(8,128)S(1)} all-gather(f32[1,12,512]{2,1,0:T(8,128)S(1)} %maximum_bitcast_fusion.3), channel_id=2, replica_groups=mesh['dp'=8,'tensor'=4] {'dp'}, dimensions={0}, use_global_device_ids=true | all-gather | bytes 221184 | tf_op jit(solution)/shard_map/all_gather | solution.py:129
  267.8 89.0 %all-gather.28.cloned.1.call-done = bf16[4096,2048]{1,0:T(8,128)(2,1)} async-done(((bf16[128,2048]{1,0:T(8,128)(2,1)}), bf16[4096,2048]{1,0:T(8,128)(2,1)}) %all-gather.28.cloned.1.call-update) | async-done | bytes 16777232 | tf_op jit(solution)/shard_map/all_gather | solution.py:131
  356.8 18.8 %multiply_convert_fusion = bf16[8,4,144,2048]{3,2,1,0:T(8,128)(2,1)} fusion(f32[8,4,144]{2,1,0:T(4,128)S(1)} %select_reduce_fusion, bf16[8,512,2048,1]{2,1,3,0:T(8,128)(2,1)} %bitcast.228, s32[8,4,512]{2,1,0:T(4,128)S(1)} %copy.133), kind=kOutput, calls=%fused_computation.3 | convolution fusion | flops 9684910080 | bytes 35735552 | tf_op jit(solution)/shard_map/sect,std->secd/dot_general | solution.py:231
  375.6 97.3 %all-gather.26.cloned.1.call-done = bf16[4096,2048]{1,0:T(8,128)(2,1)} async-done(((bf16[128,2048]{1,0:T(8,128)(2,1)}), bf16[4096,2048]{1,0:T(8,128)(2,1)}) %all-gather.26.cloned.1.call-update) | async-done | bytes 16777232 | tf_op jit(solution)/shard_map/all_gather | solution.py:224
  472.8 18.7 %convolution_convert_fusion = bf16[8,4,144,2048]{3,2,1,0:T(8,128)(2,1)} fusion(bf16[8,512,2048,1]{2,1,3,0:T(8,128)(2,1)} %bitcast.229, s32[8,4,512]{2,1,0:T(4,128)S(1)} %copy.133), kind=kOutput, calls=%fused_computation.18 | convolution fusion | flops 9675472896 | bytes 35717120 | tf_op jit(solution)/shard_map/sect,std->secd/dot_general | solution.py:225
  491.5 17.3 %fusion.11 = f32[4,8,144,352]{3,2,1,0:T(8,128)} fusion(bf16[8,4,144,2048]{3,2,1,0:T(8,128)(2,1)} %convolution_convert_fusion, bf16[4,2048,352]{1,2,0:T(8,128)(2,1)} %param.33), kind=kOutput, calls=%fused_computation.14 | convolution fusion | flops 6643777536 | bytes 31129600 | tf_op jit(solution)/shard_map/secd,edf->secf/dot_general | solution.py:241
  508.8 17.3 %fusion.13 = f32[4,8,144,352]{3,2,1,0:T(8,128)} fusion(bf16[8,4,144,2048]{3,2,1,0:T(8,128)(2,1)} %convolution_convert_fusion, bf16[4,2048,352]{1,2,0:T(8,128)(2,1)} %param.32), kind=kOutput, calls=%fused_computation.16 | convolution fusion | flops 6643777536 | bytes 31129600 | tf_op jit(solution)/shard_map/secd,edf->secf/dot_general | solution.py:238
  526.2 20.8 %fusion.23 = (bf16[8,4,144,352]{3,2,0,1:T(8,128)(2,1)}, bf16[8,4,144,352]{3,2,0,1:T(8,128)(2,1)S(1)}, bf16[8,4,144,352]{3,2,0,1:T(8,128)(2,1)}) fusion(f32[4,8,144,352]{3,2,1,0:T(8,128)} %fusion.13, f32[4,8,144,352]{3,2,1,0:T(8,128)} %fusion.11, bf16[4,352,2048]{2,1,0:T(8,128)(2,1)} %param.34, bf16[8,4,144,2048]{3,2,1,0:T(8,128)(2,1)} %multiply_convert_fusion), kind=kOutput, calls=%fused_computation.27 | convolution fusion | flops 6669729792 | bytes 47349760 | tf_op jit(solution)/shard_map/secd,efd->secf/dot_general | solution.py:260
  547.0 20.0 %fusion.40 = f32[4,8,144,2048]{3,2,0,1:T(8,128)} fusion(bf16[4,2048,352]{1,2,0:T(8,128)(2,1)} %param.32, bf16[8,4,144,352]{3,2,0,1:T(8,128)(2,1)S(1)} %get-tuple-element.28), kind=kOutput, calls=%fused_computation.47 | convolution fusion | flops 6643777536 | bytes 46759936 | tf_op jit(solution)/shard_map/azlh,zoh->azlo/dot_general | solution.py:277
  567.0 37.2 %bitcast_convert_fusion = bf16[8,512,2048]{2,1,0:T(8,128)(2,1)} fusion(f32[4,8,144,2048]{3,2,0,1:T(8,128)} %fusion.40, bf16[4,2048,352]{1,2,0:T(8,128)(2,1)} %param.33, bf16[8,4,144,352]{3,2,0,1:T(8,128)(2,1)} %get-tuple-element.27, pred[8,4,144,512]{3,2,1,0:T(8,128)(4,1)} %iota_compare_fusion.14), kind=kOutput, calls=%fused_computation.4 | convolution fusion | flops 16334716928 | bytes 65896448 | tf_op jit(solution)/shard_map/sect,secd->std/dot_general | solution.py:289
  606.3 28.3 %bitcast_convert_fusion.1 = bf16[8,512,2048]{2,1,0:T(8,128)(2,1)} fusion(f32[8,4,144]{2,1,0:T(4,128)S(1)} %copy-done.50, bf16[4,352,2048]{2,1,0:T(8,128)(2,1)} %param.34, bf16[8,4,144,352]{3,2,0,1:T(8,128)(2,1)} %get-tuple-element.29, pred[8,4,144,512]{3,2,1,0:T(8,128)(4,1)S(1)} %iota_compare_fusion.15), kind=kOutput, calls=%fused_computation.5 | convolution fusion | flops 16334716928 | bytes 28166144 | tf_op jit(solution)/shard_map/sect,secd->std/dot_general | solution.py:251
  636.1 4.6 fusion.110
  640.8 5.5 fusion.109
  646.2 6.0 multiply_convert_fusion.4
  652.2 3.9 fusion.111
  656.1 114.9 %reduce-scatter.12.cloned.1.call-done = bf16[512,2048]{1,0:T(8,128)(2,1)} async-done(((bf16[4096,2048]{1,0:T(8,128)(2,1)}), bf16[512,2048]{1,0:T(8,128)(2,1)}) %reduce-scatter.12.cloned.1.call-update) | async-done | bytes 2097168 | tf_op jit(solution)/shard_map/reduce_scatter | solution.py:292
  771.0 7.2 add_convert_fusion.2
  778.3 4.9 convolution_convert_fusion.3
  783.2 5.1 convolution_convert_fusion.2
  788.5 3.3 convolution_convert_fusion.4
  791.9 147.9 %reduce-scatter.10.cloned.1.call-done = bf16[512,2048]{1,0:T(8,128)(2,1)} async-done(((bf16[4096,2048]{1,0:T(8,128)(2,1)}), bf16[512,2048]{1,0:T(8,128)(2,1)}) %reduce-scatter.10.cloned.1.call-update) | async-done | bytes 2097168 | tf_op jit(solution)/shard_map/reduce_scatter | solution.py:254
  939.9 5.6 add_convert_fusion.4
  945.5 65.5 %all-reduce.15.cloned.1.call-done = bf16[512,2048]{1,0:T(8,128)(2,1)} async-done(((bf16[512,2048]{1,0:T(8,128)(2,1)}), bf16[512,2048]{1,0:T(8,128)(2,1)}) %all-reduce.15.cloned.1.call-update) | async-done | bytes 2097168 | tf_op jit(solution)/shard_map/psum | solution.py:303
  1011.0 3.6 multiply_reduce_fusion.2
  1034.6 3.2 add_convert_fusion.1
  1038.9 4.9 convolution_convert_fusion.5
  1043.9 3.7 convolution_convert_fusion.1
  1047.7 4.4 fusion.82
  1054.7 39.1 %reduce-scatter.24.cloned.1.call-done = bf16[256,704]{0,1:T(8,128)(2,1)} async-done(((bf16[2048,704]{0,1:T(8,128)(2,1)}), bf16[256,704]{0,1:T(8,128)(2,1)}) %reduce-scatter.24.cloned.1.call-update) | async-done | bytes 360464 | tf_op jit(solution)/shard_map/reduce_scatter | solution.py:392
  1095.7 38.7 %reduce-scatter.26.cloned.1.call-done = bf16[704,256]{1,0:T(8,128)(2,1)} async-done(((bf16[704,2048]{1,0:T(8,128)(2,1)}), bf16[704,256]{1,0:T(8,128)(2,1)}) %reduce-scatter.26.cloned.1.call-update) | async-done | bytes 360464 | tf_op jit(solution)/shard_map/reduce_scatter | solution.py:395
  1136.3 15.5 %convolution_bitcast_fusion = f32[4,2048,352]{1,2,0:T(8,128)} fusion(bf16[8,4,144,2048]{3,2,1,0:T(8,128)(2,1)} %convolution_convert_fusion, bf16[8,4,144,352]{3,2,0,1:T(8,128)(2,1)} %get-tuple-element.27), kind=kOutput, calls=%fused_computation.50 | convolution fusion | flops 6643777536 | bytes 33652736 | tf_op jit(solution)/shard_map/zxmi,zxmh->xih/dot_general | solution.py:274
  1151.8 15.2 %convolution_bitcast_fusion.1 = f32[4,2048,352]{1,2,0:T(8,128)} fusion(bf16[8,4,144,2048]{3,2,1,0:T(8,128)(2,1)} %convolution_convert_fusion, bf16[8,4,144,352]{3,2,0,1:T(8,128)(2,1)} %copy-done.18), kind=kOutput, calls=%fused_computation.51 | convolution fusion | flops 6643777536 | bytes 33652736 | tf_op jit(solution)/shard_map/zxmi,zxmh->xih/dot_general | solution.py:271
  1166.9 15.3 %fusion.42 = f32[4,352,2048]{2,1,0:T(8,128)} fusion(bf16[8,4,144,352]{3,2,0,1:T(8,128)(2,1)} %get-tuple-element.29, bf16[8,4,144,2048]{3,2,1,0:T(8,128)(2,1)} %multiply_convert_fusion), kind=kOutput, calls=%fused_computation.49 | convolution fusion | flops 6643777536 | bytes 33652736 | tf_op jit(solution)/shard_map/secf,secd->efd/dot_general | solution.py:263
  1187.7 86.5 %all-reduce.17.cloned.1.call-done = (bf16[512,2048]{1,0:T(8,128)(2,1)}, bf16[512,2048]{1,0:T(8,128)(2,1)}) async-done(((bf16[512,2048]{1,0:T(8,128)(2,1)}, bf16[512,2048]{1,0:T(8,128)(2,1)}), (bf16[512,2048]{1,0:T(8,128)(2,1)}, bf16[512,2048]{1,0:T(8,128)(2,1)})) %all-reduce.17.cloned.1.call-update) | async-done | bytes 4194320 | tf_op jit(solution)/shard_map/psum | solution.py:257
  1277.7 3.6 convert_multiply_fusion
  1281.4 40.4 %all-reduce.6 = (f32[2048]{0:T(1024)S(1)}, f32[512]{0:T(512)S(1)}, f32[2048]{0:T(1024)S(1)}) all-reduce(f32[2048]{0:T(1024)S(1)} %fusion.70, f32[512]{0:T(512)S(1)} %get-tuple-element.15, f32[2048]{0:T(1024)S(1)} %fusion.69), channel_id=5, replica_groups=mesh['dp'=8,'tensor'=4] {'dp','tensor'}, use_global_device_ids=true, to_apply=%region_22.23.clone | all-reduce | flops 4608 | bytes 36864
  1325.3 6.1 multiply_add_fusion
  1331.5 22.6 %reduce-scatter.14.cloned.1.call-done = bf16[256,768]{1,0:T(8,128)(2,1)} async-done(((bf16[2048,768]{1,0:T(8,128)(2,1)}), bf16[256,768]{1,0:T(8,128)(2,1)}) %reduce-scatter.14.cloned.1.call-update) | async-done | bytes 393232 | tf_op jit(solution)/shard_map/reduce_scatter | solution.py:380
  1356.0 145.1 %reduce-scatter.16.cloned.1.call-done = f32[64,576]{1,0:T(8,128)} async-done(((f32[2048,576]{1,0:T(8,128)}), f32[64,576]{1,0:T(8,128)}) %reduce-scatter.16.cloned.1.call-update) | async-done | bytes 147472 | tf_op jit(solution)/shard_map/reduce_scatter | solution.py:400
  (265 shorter events, 91.7 us)
Async XLA Ops:
  7.2 64.5 %all-gather.12.cloned.1.call-start = ((), (), s32[]{:S(2)}) async-start(), calls=%async_computation.9 | async-start | bytes 2703360 | tf_op jit(solution)/shard_map/all_gather | solution.py:141
  7.9 86.4 %all-gather.14.cloned.1.call-start = ((), (), s32[]{:S(2)}) async-start(), calls=%async_computation.10 | async-start | bytes 1179648 | tf_op jit(solution)/shard_map/all_gather | solution.py:134
  8.7 125.2 %all-gather.16.cloned.1.call-start = ((), (), s32[]{:S(2)}) async-start(), calls=%async_computation.11 | async-start | bytes 3538944 | tf_op jit(solution)/shard_map/all_gather | solution.py:133
  9.4 155.5 %all-gather.18.cloned.1.call-start = ((), (), s32[]{:S(2)}) async-start(), calls=%async_computation.12 | async-start | bytes 2359296 | tf_op jit(solution)/shard_map/all_gather | solution.py:135
  10.0 227.8 %all-reduce.13.cloned.1.call-start = ((), (), s32[]{:S(2)}) async-start(), calls=%async_computation.13 | async-start | bytes 4194304 | tf_op jit(solution)/shard_map/psum | solution.py:206
  13.3 91.4 %copy-start.51 = (f32[512]{0:T(512)}, f32[512]{0:T(512)S(1)}, u32[]{:S(2)}) copy-start(f32[512]{0:T(512)S(1)} %subtract_convert_fusion.2) | copy-start | bytes 6148
  15.4 60.2 %copy-start.58 = (f32[512]{0:T(512)}, f32[512]{0:T(512)S(1)}, u32[]{:S(2)}) copy-start(f32[512]{0:T(512)S(1)} %add_rsqrt_fusion.2) | copy-start | bytes 6148
  60.3 34.0 %copy-start.55 = (f32[512]{0:T(512)}, f32[512]{0:T(512)S(1)}, u32[]{:S(2)}) copy-start(f32[512]{0:T(512)S(1)} %convert_element_type.192) | copy-start | bytes 6148
  60.4 73.5 %copy-start.47 = (f32[2048]{0:T(1024)}, f32[2048]{0:T(1024)S(1)}, u32[]{:S(2)}) copy-start(f32[2048]{0:T(1024)S(1)} %convert_element_type.190) | copy-start | bytes 24580
  75.6 29.1 %copy-start.10 = (f32[512,576]{0,1:T(8,128)}, f32[512,576]{0,1:T(8,128)S(1)}, u32[]{:S(2)}) copy-start(f32[512,576]{0,1:T(8,128)S(1)} %fusion.104) | copy-start | bytes 3538948
  76.5 57.4 %copy-start.2 = (bf16[512,2048]{1,0:T(8,128)(2,1)S(1)}, bf16[512,2048]{1,0:T(8,128)(2,1)}, u32[]{:S(2)}) copy-start(bf16[512,2048]{1,0:T(8,128)(2,1)} %param.18) | copy-start | bytes 6291460
  106.3 31.4 %copy-start.32 = (f32[512,32]{0,1:T(8,128)S(1)}, f32[512,32]{0,1:T(8,128)}, u32[]{:S(2)}) copy-start(f32[512,32]{0,1:T(8,128)} %get-tuple-element.50) | copy-start | bytes 196612
  106.3 31.4 %copy-start.42 = (f32[512,32]{0,1:T(8,128)S(1)}, f32[512,32]{0,1:T(8,128)}, u32[]{:S(2)}) copy-start(f32[512,32]{0,1:T(8,128)} %get-tuple-element.49) | copy-start | bytes 196612
  106.3 31.5 %copy-start.14 = (bf16[512,4,128]{2,1,0:T(4,128)(2,1)S(1)}, bf16[512,4,128]{2,1,0:T(4,128)(2,1)}, u32[]{:S(2)}) copy-start(bf16[512,4,128]{2,1,0:T(4,128)(2,1)} %get-tuple-element.40) | copy-start | bytes 1572868
  143.3 27.7 %copy-start.34 = (bf16[4,128,512]{2,1,0:T(8,128)(2,1)}, bf16[4,128,512]{2,1,0:T(8,128)(2,1)S(1)}, u32[]{:S(2)}) copy-start(bf16[4,128,512]{2,1,0:T(8,128)(2,1)S(1)} %convolution_convert_fusion.11) | copy-start | bytes 1572868
  164.9 6.7 copy-start.62
  169.1 187.7 %all-gather.28.cloned.1.call-start = ((), (), s32[]{:S(2)}) async-start(), calls=%async_computation.19 | async-start | bytes 17301504 | tf_op jit(solution)/shard_map/all_gather | solution.py:131
  171.0 301.8 %all-gather.26.cloned.1.call-start = ((), (), s32[]{:S(2)}) async-start(), calls=%async_computation.17 | async-start | bytes 17301504 | tf_op jit(solution)/shard_map/all_gather | solution.py:224
  171.6 71.9 %copy-start.45 = (f32[2048]{0:T(1024)}, f32[2048]{0:T(1024)S(1)}, u32[]{:S(2)}) copy-start(f32[2048]{0:T(1024)S(1)} %convert_element_type.202) | copy-start | bytes 24580
  240.3 7.5 copy-start.60
  240.3 7.5 copy-start.61
  245.6 389.4 %all-gather.22.cloned.1.call-start = ((), (), s32[]{:S(2)}) async-start(), calls=%async_computation.15 | async-start | bytes 3244032 | tf_op jit(solution)/shard_map/all_gather | solution.py:137
  246.4 394.4 %all-gather.20.cloned.1.call-start = ((), (), s32[]{:S(2)}) async-start(), calls=%async_computation.14 | async-start | bytes 3244032 | tf_op jit(solution)/shard_map/all_gather | solution.py:136
  247.1 399.1 %all-gather.24.cloned.1.call-start = ((), (), s32[]{:S(2)}) async-start(), calls=%async_computation.16 | async-start | bytes 3244032 | tf_op jit(solution)/shard_map/all_gather | solution.py:138
  247.7 523.3 %reduce-scatter.12.cloned.1.call-start = ((), (), s32[]{:S(2)}) async-start(), calls=%async_computation.20 | async-start | bytes 18874368 | tf_op jit(solution)/shard_map/reduce_scatter | solution.py:292
  263.7 209.2 %copy-start.28 = (s32[8,4,512]{2,1,0:T(4,128)}, s32[8,4,512]{2,1,0:T(4,128)S(1)}, u32[]{:S(2)}) copy-start(s32[8,4,512]{2,1,0:T(4,128)S(1)} %copy.133) | copy-start | bytes 196612
  267.8 107.7 %copy-start.49 = (f32[8,4,144]{2,1,0:T(4,128)}, f32[8,4,144]{2,1,0:T(4,128)S(1)}, u32[]{:S(2)}) copy-start(f32[8,4,144]{2,1,0:T(4,128)S(1)} %select_reduce_fusion) | copy-start | bytes 55300
  547.0 20.0 %copy-start.18 = (bf16[8,4,144,352]{3,2,0,1:T(8,128)(2,1)}, bf16[8,4,144,352]{3,2,0,1:T(8,128)(2,1)S(1)}, u32[]{:S(2)}) copy-start(bf16[8,4,144,352]{3,2,0,1:T(8,128)(2,1)S(1)} %get-tuple-element.28) | copy-start | bytes 9732100
  604.2 335.7 %reduce-scatter.10.cloned.1.call-start = ((), (), s32[]{:S(2)}) async-start(), calls=%async_computation.18 | async-start | bytes 18874368 | tf_op jit(solution)/shard_map/reduce_scatter | solution.py:254
  634.6 376.4 %all-reduce.15.cloned.1.call-start = ((), (), s32[]{:S(2)}) async-start(), calls=%async_computation.21 | async-start | bytes 4194304 | tf_op jit(solution)/shard_map/psum | solution.py:303
  640.8 5.5 copy-start.19
  646.2 6.0 copy-start.22
  778.2 274.6 %reduce-scatter.22.cloned.1.call-start = ((), (), s32[]{:S(2)}) async-start(), calls=%async_computation.26 | async-start | bytes 3244032 | tf_op jit(solution)/shard_map/reduce_scatter | solution.py:389
  783.2 310.6 %reduce-scatter.24.cloned.1.call-start = ((), (), s32[]{:S(2)}) async-start(), calls=%async_computation.27 | async-start | bytes 3244032 | tf_op jit(solution)/shard_map/reduce_scatter | solution.py:392
  788.3 346.1 %reduce-scatter.26.cloned.1.call-start = ((), (), s32[]{:S(2)}) async-start(), calls=%async_computation.28 | async-start | bytes 3244032 | tf_op jit(solution)/shard_map/reduce_scatter | solution.py:395
  791.9 219.1 %copy-start.46 = (f32[2048]{0:T(1024)S(1)}, f32[2048]{0:T(1024)}, u32[]{:S(2)}) copy-start(f32[2048]{0:T(1024)} %copy-done.45) | copy-start | bytes 24580
  791.9 394.1 %reduce-scatter.18.cloned.1.call-start = ((), (), s32[]{:S(2)}) async-start(), calls=%async_computation.24 | async-start | bytes 1179648 | tf_op jit(solution)/shard_map/reduce_scatter | solution.py:383
  945.5 69.1 %copy-start.54 = (f32[512]{0:T(512)S(1)}, f32[512]{0:T(512)}, u32[]{:S(2)}) copy-start(f32[512]{0:T(512)} %copy-done.53) | copy-start | bytes 6148
  1011.0 4.7 copy-start.5
  1017.3 4.9 copy-start.9
  1029.5 244.7 %all-reduce.17.cloned.1.call-start = ((), (), s32[]{:S(2)}) async-start(), calls=%async_computation.29 | async-start | bytes 8388608 | tf_op jit(solution)/shard_map/psum | solution.py:257
  1037.9 6.0 copy-start.3
  1037.9 6.0 copy-start.31
  1037.9 6.0 copy-start.48
  1037.9 6.0 copy-start.59
  1037.9 285.6 %reduce-scatter.20.cloned.1.call-start = ((), (), s32[]{:S(2)}) async-start(), calls=%async_computation.25 | async-start | bytes 2359296 | tf_op jit(solution)/shard_map/reduce_scatter | solution.py:386
  1043.8 310.2 %reduce-scatter.14.cloned.1.call-start = ((), (), s32[]{:S(2)}) async-start(), calls=%async_computation.22 | async-start | bytes 3538944 | tf_op jit(solution)/shard_map/reduce_scatter | solution.py:380
  1047.6 453.5 %reduce-scatter.16.cloned.1.call-start = ((), (), s32[]{:S(2)}) async-start(), calls=%async_computation.23 | async-start | bytes 5406720 | tf_op jit(solution)/shard_map/reduce_scatter | solution.py:400
  (40 other events, 88.9 us)
Sparse Core Ops, SparseCore 0:
  10.9 60.7 all-gather.11
  73.3 21.0 all-gather.13
  96.0 37.8 all-gather.15
  135.3 29.5 all-gather.17
  169.2 68.4 all-reduce.12
  241.0 115.7 all-gather.27
  360.2 112.5 all-gather.25
  474.4 35.2 all-gather.21
  511.3 35.2 all-gather.19
  548.0 35.2 all-gather.23
  604.3 166.6 reduce-scatter.11
  773.2 166.6 reduce-scatter.9
  943.0 67.9 all-reduce.14
  1013.7 39.0 reduce-scatter.21
  1055.6 38.2 reduce-scatter.23
  1096.0 38.3 reduce-scatter.25
  1136.5 31.7 reduce-scatter.17
  1172.3 101.8 all-reduce.16
  1276.5 36.4 reduce-scatter.19
  1315.1 38.9 reduce-scatter.13
  1356.9 144.1 reduce-scatter.15
